TPU v7x, 128 devices: a whole 4x4x4 slice. The times are simulated.
128 devices in a mesh: sa: 8 (over x, core), an: 16 (over y, z).
Axes of the slice: x: 4, y: 4, z: 4, core: 2. Of those that a mesh axis runs over, the one named last changes fastest.
Arguments:
- decoder_states: bfloat16 [8192, 4096], P('sa', 'an'), may hold values from -170 to 170
- w_query: bfloat16 [4096, 4096], P(None, 'an'), may hold values from -0.09375 to 0.09375
- w_key: bfloat16 [1024, 4096], P(None, 'an'), may hold values from -0.1875 to 0.1875
- w_value: bfloat16 [1024, 4096], P(None, 'an'), may hold values from -0.1875 to 0.1875
- w_out: bfloat16 [4096, 4096], P('an'), may hold values from -0.375 to 0.375
- enc_up: bfloat16 [1024, 4096], replicated, may hold values from -0.1875 to 0.1875
- enc_down: bfloat16 [4096, 1024], replicated, may hold values from -0.09375 to 0.09375
- neighbour_inputs: bfloat16 [1024, 128, 1024], P(('sa', 'an')), may hold values from -6 to 6
- requests: int32 [256], P('sa'), may hold values from 0 to 127, as said below
Outputs:
- cross_output: bfloat16 [8192, 4096], P('sa', 'an')
Inputs may be any that keep to these rules, and one draw needn't show every extreme that they name: Within each block of 32 requests (one index of sa) the owner of a request is its value // 8; no owner receives more than 4 requests of a block and no more than 2 distinct neighbours of one owner are requested in a block; in every block some owner receives exactly 4 requests, 2 of them distinct. A neighbour may be requested several times.
All inputs are finite; a program needn't handle non-finite values.
Results may differ from a plain program's by a relative error of at most 0.01.
The roundings to bfloat16 on the way count: a program that leaves them out, or rounds other values in their place, can miss the bound.
Values may be sent and summed in bfloat16 or wider, within the bound.
A program may use at most 128 MiB of HBM per device.

v0:
```python
import jax
import jax.numpy as jnp
from jax import lax
from jax.sharding import PartitionSpec as P

D = 4096
HEADS = 32
GROUP = 64
NEIGH = 2
EPS = 1e-06


def encode(rows, enc_up, enc_down):
    wide = rows.astype(jnp.float32)
    square = jnp.mean(wide * wide, axis=-1, keepdims=True)
    normed = (wide * lax.rsqrt(square + EPS)).astype(jnp.bfloat16)
    hidden = jax.nn.gelu(
        jnp.dot(normed, enc_up, preferred_element_type=jnp.float32), approximate=False
    ).astype(jnp.bfloat16)
    return (wide + jnp.dot(hidden, enc_down, preferred_element_type=jnp.float32)).astype(
        jnp.bfloat16
    )


def shards(
    decoder_states, w_query, w_key, w_value, w_out, enc_up, enc_down, neighbour_inputs, requests
):
    owner_total = lax.axis_size("an")
    position = lax.axis_index("an")
    tok_rows, local_width = decoder_states.shape
    head_dim = D // HEADS
    heads_here = local_width // head_dim
    scale = float(head_dim) ** (-0.5)
    total_requests = requests.shape[0]
    per_owner = total_requests // owner_total
    nb_own = neighbour_inputs.shape[0]
    span = neighbour_inputs.shape[1]
    owner = requests // nb_own
    local_id = requests % nb_own
    owner_range = jnp.arange(owner_total, dtype=jnp.int32)
    local_range = jnp.arange(nb_own, dtype=jnp.int32)
    hits = (owner[:, None, None] == owner_range[None, :, None]) & (
        local_id[:, None, None] == local_range[None, None, :]
    )
    present = jnp.any(hits, axis=0).astype(jnp.int32)
    ranked = jnp.cumsum(present, axis=1) - present
    slot_of_request = owner * per_owner + ranked[owner, local_id]
    my_present = jnp.sum(jnp.where(owner_range[:, None] == position, present, 0), axis=0)
    my_rank = jnp.sum(jnp.where(owner_range[:, None] == position, ranked, 0), axis=0)
    chosen_mask = (my_present[:, None] == 1) & (
        my_rank[:, None] == jnp.arange(per_owner, dtype=jnp.int32)[None, :]
    )
    local_of_slot = jnp.sum(jnp.where(chosen_mask, local_range[:, None], 0), axis=0)
    rows = w_query
    queries = jnp.dot(
        lax.all_gather(decoder_states, "an", axis=1, tiled=True),
        rows,
        preferred_element_type=jnp.float32,
    )
    chosen = neighbour_inputs[local_of_slot].reshape(per_owner * span, neighbour_inputs.shape[2])
    encoded = encode(chosen, enc_up, enc_down)
    both_weights = jnp.concatenate([w_key, w_value], axis=1)
    projected = jnp.dot(
        lax.all_gather(encoded, "an", axis=0, tiled=True),
        both_weights,
        preferred_element_type=jnp.float32,
    ).astype(jnp.bfloat16)
    projected = projected.reshape(owner_total * per_owner, span, 2 * local_width)
    groups = tok_rows // GROUP
    selected = projected[slot_of_request].reshape(groups, NEIGH * span, 2 * local_width)
    keys = selected[:, :, :local_width].reshape(groups, NEIGH * span, heads_here, head_dim)
    values = selected[:, :, local_width:].reshape(groups, NEIGH * span, heads_here, head_dim)
    queries = queries.astype(jnp.bfloat16).reshape(groups, GROUP, heads_here, head_dim)
    scores = (
        jnp.einsum("cqhd,ckhd->chqk", queries, keys, preferred_element_type=jnp.float32) * scale
    )
    top = jnp.max(scores, axis=-1, keepdims=True)
    weights = jnp.exp(scores - top)
    probs = (weights / jnp.sum(weights, axis=-1, keepdims=True)).astype(jnp.bfloat16)
    attended = jnp.einsum(
        "chqk,ckhd->cqhd", probs, values, preferred_element_type=jnp.float32
    ).astype(jnp.bfloat16)
    attended = attended.reshape(tok_rows, local_width)
    column_block = lax.all_to_all(w_out, "an", split_axis=1, concat_axis=0, tiled=True)
    rows = column_block
    summed = jnp.dot(
        lax.all_gather(attended, "an", axis=1, tiled=True), rows, preferred_element_type=jnp.float32
    )
    return summed.astype(jnp.bfloat16)


def solution(mesh):
    placed = (
        P("sa", "an"),
        P(None, "an"),
        P(None, "an"),
        P(None, "an"),
        P("an", None),
        P(),
        P(),
        P(("sa", "an"), None, None),
        P("sa"),
    )
    return jax.shard_map(
        shards, mesh=mesh, in_specs=placed, out_specs=P("sa", "an"), check_vma=False
    )
```

profile of v0, /device:TPU:0, one launch (start us, length us, event | category | flops | bytes accessed | tf_op | source)
XLA Modules:
  0.0 301.6 jit_solution(9796901206107320811)
XLA Ops:
  6.5 0.0 copy-start
  6.5 0.0 all-gather.4.cloned.1.call-start
  6.5 0.8 fusion.66
  7.4 0.4 and_reduce_fusion
  7.8 0.2 reduce_window_sum.11
  7.9 0.1 select_reduce_fusion
  8.0 0.1 fusion.62
  8.2 0.0 copy-done
  8.2 0.6 gather_fusion
  8.8 0.2 multiply_reduce_fusion.1
  9.0 0.2 fusion.54
  9.1 0.0 copy-start.4
  9.1 0.0 copy-start.5
  9.2 17.1 %fusion.47 = bf16[256,1024]{1,0:T(8,128)(2,1)} fusion(bf16[4096,1024]{1,0:T(8,128)(2,1)} %param.15, bf16[256,1024]{1,0:T(8,128)(2,1)S(1)} %fusion.54, bf16[1024,4096]{1,0:T(8,128)(2,1)} %param.14, bf16[256,1024]{1,0:T(8,128)(2,1)S(1)} %bitcast.39), kind=kOutput, calls=%fused_computation.63 | convolution fusion | flops 4363911168 | bytes 18350080 | tf_op jit(solution)/shard_map/dot_general | solution.py:20
  26.3 0.0 all-gather.4.cloned.1.call-update
  26.3 0.0 all-gather.6.cloned.1.call-start
  26.3 0.7 all-gather.6.cloned.1.call-update
  27.0 0.2 all-gather.8.cloned.1.call-start
  27.3 0.7 gather_fusion.1
  28.0 71.9 %all-gather.4.cloned.1.call-done = bf16[4096,1024]{1,0:T(8,128)(2,1)} async-done(((bf16[256,1024]{1,0:T(8,128)(2,1)}), bf16[4096,1024]{1,0:T(8,128)(2,1)}) %all-gather.4.cloned.1.call-update) | async-done | bytes 8388624 | tf_op jit(solution)/shard_map/all_gather | solution.py:64
  99.9 0.0 copy-done.4
  99.9 0.0 copy-done.5
  99.9 9.6 %convolution_convert_fusion = bf16[4096,512]{1,0:T(8,128)(2,1)} fusion(bf16[4096,1024]{1,0:T(8,128)(2,1)} %all-gather.4.cloned.1.call-done, bf16[1024,256]{1,0:T(8,128)(2,1)S(1)} %copy-done.4, bf16[1024,256]{1,0:T(8,128)(2,1)S(1)} %copy-done.5), kind=kOutput, calls=%fused_computation.5 | convolution fusion | flops 4299161600 | bytes 13631488 | tf_op jit(solution)/shard_map/dot_general | solution.py:63
  109.5 5.2 %gather_fusion.2 = bf16[32,128,512]{2,1,0:T(8,128)(2,1)} fusion(bf16[32,128,512]{2,1,0:T(8,128)(2,1)} %bitcast.40, s32[1024]{0:T(1024)S(1)} %pad_clamp_fusion), kind=kCustom, calls=%fused_computation.2 | custom fusion | bytes 8388736 | tf_op jit(solution)/shard_map/gather | solution.py:70
  114.6 4.0 %fusion.104 = (bf16[16,256,256]{2,1,0:T(8,128)(2,1)}, bf16[16,256,256]{2,1,0:T(8,128)(2,1)S(1)}) fusion(bf16[16,256,512]{2,1,0:T(8,128)(2,1)} %bitcast.35), kind=kLoop, calls=%fused_computation.137 | loop fusion | bytes 8388608 | tf_op jit(solution)/shard_map/slice | solution.py:71
  118.7 2.4 copy.23
  121.1 2.8 copy.24
  123.9 55.0 %all-gather.6.cloned.1.call-done = bf16[1024,4096]{1,0:T(8,128)(2,1)} async-done(((bf16[1024,256]{1,0:T(8,128)(2,1)}), bf16[1024,4096]{1,0:T(8,128)(2,1)}) %all-gather.6.cloned.1.call-update) | async-done | bytes 8388624 | tf_op jit(solution)/shard_map/all_gather | solution.py:56
  179.0 6.3 %convolution_convert_fusion.3 = bf16[1024,256]{1,0:T(8,128)(2,1)S(1)} fusion(bf16[1024,4096]{1,0:T(8,128)(2,1)} %all-gather.6.cloned.1.call-done, bf16[4096,256]{1,0:T(8,128)(2,1)} %param.10), kind=kOutput, calls=%fused_computation.62 | convolution fusion | flops 2147745792 | bytes 11010048 | tf_op jit(solution)/shard_map/dot_general | solution.py:55
  185.3 0.1 reshape.115
  185.4 0.4 fusion.56
  185.8 0.0 copy-start.3
  185.8 0.8 fusion.105
  186.6 0.6 copy-done.3
  187.2 0.0 copy-start.2
  187.2 6.0 %fusion.50 = bf16[16,64,2,128]{3,1,2,0:T(8,128)(2,1)S(1)} fusion(bf16[16,256,2,128]{1,3,2,0:T(8,128)(2,1)} %bitcast.41, f32[16,2,64]{2,1,0:T(2,128)S(1)} %fusion.105, f32[16,2,64,256]{3,2,1,0:T(8,128)} %copy-done.3), kind=kOutput, calls=%fused_computation.64 | convolution fusion | flops 136579328 | bytes 4726784 | tf_op jit(solution)/shard_map/chqk,ckhd->cqhd/dot_general | solution.py:80
  193.2 0.6 copy.28
  193.8 0.9 copy.37
  194.6 0.0 all-gather.8.cloned.1.call-update
  194.7 0.0 copy-done.2
  194.7 2.5 copy.29
  197.2 40.1 %all_to_all.19 = bf16[256,16,256]{0,2,1:T(8,128)(2,1)S(1)} all-to-all(bf16[256,16,256]{0,2,1:T(8,128)(2,1)} %bitcast.38), channel_id=1, replica_groups=mesh['sa'=8,'an'=16] {'an'}, dimensions={1} | all-to-all | bytes 4194304 | tf_op jit(solution)/shard_map/all_to_all | solution.py:84
  237.3 2.4 copy.30
  239.7 48.1 %all-gather.8.cloned.1.call-done = bf16[1024,4096]{1,0:T(8,128)(2,1)} async-done(((bf16[1024,256]{1,0:T(8,128)(2,1)}), bf16[1024,4096]{1,0:T(8,128)(2,1)}) %all-gather.8.cloned.1.call-update) | async-done | bytes 8388624 | tf_op jit(solution)/shard_map/all_gather | solution.py:87
  287.9 0.0 copy-start.1
  287.9 7.2 %convolution_convert_fusion.1 = bf16[1024,256]{1,0:T(8,128)(2,1)} fusion(bf16[1024,4096]{1,0:T(8,128)(2,1)} %all-gather.8.cloned.1.call-done, bf16[4096,256]{1,0:T(8,128)(2,1)} %bitcast.42), kind=kOutput, calls=%fused_computation.60 | convolution fusion | flops 2147745792 | bytes 11010048 | tf_op jit(solution)/shard_map/dot_general | solution.py:86
  295.1 0.0 copy-done.1
  (10 shorter events, 0.1 us)
Async XLA Ops:
  6.5 1.6 copy-start
  6.5 93.3 %all-gather.4.cloned.1.call-start = ((), (), s32[]{:S(2)}) async-start(), calls=%async_computation.1 | async-start | bytes 8912896 | tf_op jit(solution)/shard_map/all_gather | solution.py:64
  9.1 90.7 %copy-start.4 = (bf16[1024,256]{1,0:T(8,128)(2,1)S(1)}, bf16[1024,256]{1,0:T(8,128)(2,1)}, u32[]{:S(2)}) copy-start(bf16[1024,256]{1,0:T(8,128)(2,1)} %param.12) | copy-start | bytes 1572868
  9.1 90.7 %copy-start.5 = (bf16[1024,256]{1,0:T(8,128)(2,1)S(1)}, bf16[1024,256]{1,0:T(8,128)(2,1)}, u32[]{:S(2)}) copy-start(bf16[1024,256]{1,0:T(8,128)(2,1)} %param.11) | copy-start | bytes 1572868
  26.3 152.7 %all-gather.6.cloned.1.call-start = ((), (), s32[]{:S(2)}) async-start(), calls=%async_computation.2 | async-start | bytes 8912896 | tf_op jit(solution)/shard_map/all_gather | solution.py:56
  27.0 260.8 %all-gather.8.cloned.1.call-start = ((), (), s32[]{:S(2)}) async-start(), calls=%async_computation.3 | async-start | bytes 8912896 | tf_op jit(solution)/shard_map/all_gather | solution.py:87
  185.8 1.4 copy-start.3
  187.2 7.5 %copy-start.2 = (bf16[256,4096]{1,0:T(8,128)(2,1)S(1)}, bf16[256,4096]{1,0:T(8,128)(2,1)}, u32[]{:S(2)}) copy-start(bf16[256,4096]{1,0:T(8,128)(2,1)} %param.13) | copy-start | bytes 6291460
  287.9 7.3 %copy-start.1 = (bf16[8,128,1024]{2,1,0:T(8,128)(2,1)S(1)}, bf16[8,128,1024]{2,1,0:T(8,128)(2,1)}, u32[]{:S(2)}) copy-start(bf16[8,128,1024]{2,1,0:T(8,128)(2,1)} %param.16) | copy-start | bytes 6291460
Sparse Core Ops, SparseCore 0:
  26.4 73.4 all-gather.3
  102.0 76.9 all-gather.5
  194.8 93.0 all-gather.7
where the time goes:
time: 302 us
  waiting for transfers between devices  176 us (58%)
  matrix products  46.7 us (15%)
  blocking collectives  40.1 us (13%)
  local copies, waits for them, and re-layouts  22.9 us (8%)
  between operations  13.2 us (4%)
    all_gather x1, waiting for transfers between devices, shards(): lax.all_gather(encoded, 'an', axis=0, tiled=True)  71.9 us
    all_gather x1, waiting for transfers between devices, shards(): lax.all_gather(decoder_states, 'an', axis=1, tiled=True)  55 us
    all_gather x1, waiting for transfers between devices, shards(): lax.all_gather(attended, 'an', axis=1, tiled=True)  48.1 us
    all_to_all x1, blocking collectives, shards(): lax.all_to_all(w_out, 'an', split_axis=1, concat_axis=0, tiled=True)  40.1 us
    dot_general x1, matrix products, encode(): jnp.dot(hidden, enc_down, preferred_element_type=jnp.float32)  17.1 us
    dot_general x1, matrix products, shards(): jnp.dot(lax.all_gather(encoded, 'an', axis=0, tiled=True), both_weights,...  9.59 us
    dot_general x1, matrix products, shards(): jnp.dot(lax.all_gather(attended, 'an', axis=1, tiled=True), rows, preferr...  7.25 us
    slice x2, local copies, waits for them, and re-layouts, shards(): selected[:, :, :local_width]  6.87 us
  transfers between devices with their start and end apart: 3, of which 3 were waited for; matrix products, arithmetic and copies ran while one was open for 10% of the time, Pallas kernels for 0%

commit v1 on v0

--- a/solution.py
+++ b/solution.py
@@ -8,6 +8,11 @@
 GROUP = 64
 NEIGH = 2
 EPS = 1e-06
+
+
+def swapped_in(x, axis, dim):
+    repeated = jnp.stack([x] * lax.axis_size(axis))
+    return jnp.concatenate(lax.all_to_all(repeated, axis, 0, 0), axis=dim)
 
 
 def encode(rows, enc_up, enc_down):
@@ -52,11 +57,7 @@
     )
     local_of_slot = jnp.sum(jnp.where(chosen_mask, local_range[:, None], 0), axis=0)
     rows = w_query
-    queries = jnp.dot(
-        lax.all_gather(decoder_states, "an", axis=1, tiled=True),
-        rows,
-        preferred_element_type=jnp.float32,
-    )
+    queries = jnp.dot(swapped_in(decoder_states, "an", 1), rows, preferred_element_type=jnp.float32)
     chosen = neighbour_inputs[local_of_slot].reshape(per_owner * span, neighbour_inputs.shape[2])
     encoded = encode(chosen, enc_up, enc_down)
     both_weights = jnp.concatenate([w_key, w_value], axis=1)

time: 302 us -> 356 us (1.18)
  waiting for transfers between devices: 176 us -> 214 us
  starting transfers between devices: 0.26 us -> 8.57 us
  local copies, waits for them, and re-layouts: 22.9 us -> 27 us
    all_to_all x0 -> x1, waiting for transfers between devices: none -> 153 us  [swapped_in(): return jnp.concatenate(lax.all_to_all(repeated, axis, 0, 0), axis=dim)]
    all_gather x1, waiting for transfers between devices: 71.9 us -> 13 us  [shards(): lax.all_gather(encoded, 'an', axis=0, tiled=True)]
    all_gather x1 -> x0, waiting for transfers between devices: 55 us -> none  [shards(): lax.all_gather(decoder_states, 'an', axis=1, tiled=True)]
    all_to_all x0 -> x1, starting transfers between devices: none -> 8.34 us  [swapped_in(): return jnp.concatenate(lax.all_to_all(repeated, axis, 0, 0), axis=dim)]
    another operation x0 -> x1, local copies, waits for them, and re-layouts: none -> 4.3 us  [swapped_in(): repeated = jnp.stack([x] * lax.axis_size(axis))]
  transfers between devices with their start and end apart: 3 -> 3, of which waited for: 3 -> 3; matrix products, arithmetic and copies ran while one was open for 10% -> 5% of each run, Pallas kernels for 0% -> 0%
where the time goes in v1:
time: 356 us
  waiting for transfers between devices  214 us (60%)
  matrix products  46.7 us (13%)
  blocking collectives  43.1 us (12%)
  local copies, waits for them, and re-layouts  27 us (8%)
  between operations  13.5 us (4%)
  starting transfers between devices  8.57 us (2%)
    all_to_all x1, waiting for transfers between devices, swapped_in(): return jnp.concatenate(lax.all_to_all(repeated, axis, 0, 0), axis=dim)  153 us
    all_gather x1, waiting for transfers between devices, shards(): lax.all_gather(attended, 'an', axis=1, tiled=True)  47.9 us
    all_to_all x1, blocking collectives, shards(): lax.all_to_all(w_out, 'an', split_axis=1, concat_axis=0, tiled=True)  43.1 us
    dot_general x1, matrix products, encode(): jnp.dot(hidden, enc_down, preferred_element_type=jnp.float32)  17.1 us
    all_gather x1, waiting for transfers between devices, shards(): lax.all_gather(encoded, 'an', axis=0, tiled=True)  13 us
    dot_general x1, matrix products, shards(): jnp.dot(lax.all_gather(encoded, 'an', axis=0, tiled=True), both_weights,...  10.1 us
    all_to_all x1, starting transfers between devices, swapped_in(): return jnp.concatenate(lax.all_to_all(repeated, axis, 0, 0), axis=dim)  8.34 us
    dot_general x1, matrix products, shards(): jnp.dot(lax.all_gather(attended, 'an', axis=1, tiled=True), rows, preferr...  7.25 us
  transfers between devices with their start and end apart: 3, of which 3 were waited for; matrix products, arithmetic and copies ran while one was open for 5% of the time, Pallas kernels for 0%

profile of v1, /device:TPU:0, one launch (start us, length us, event | category | flops | bytes accessed | tf_op | source)
XLA Modules:
  0.0 355.9 jit_solution(6922819117377517457)
XLA Ops:
  6.5 0.0 copy-start
  6.5 0.0 all-gather.3.cloned.1.call-start
  6.5 0.8 fusion.66
  7.4 0.4 and_reduce_fusion
  7.8 0.2 reduce_window_sum.11
  7.9 0.1 select_reduce_fusion
  8.0 0.1 fusion.62
  8.2 0.0 copy-done
  8.2 0.6 gather_fusion
  8.8 0.2 multiply_reduce_fusion.1
  9.0 0.2 fusion.54
  9.1 0.0 copy-start.5
  9.1 17.1 %fusion.47 = bf16[256,1024]{1,0:T(8,128)(2,1)} fusion(bf16[4096,1024]{1,0:T(8,128)(2,1)} %param.15, bf16[256,1024]{1,0:T(8,128)(2,1)S(1)} %fusion.54, bf16[1024,4096]{1,0:T(8,128)(2,1)} %param.14, bf16[256,1024]{1,0:T(8,128)(2,1)S(1)} %bitcast.42), kind=kOutput, calls=%fused_computation.63 | convolution fusion | flops 4363911168 | bytes 18350080 | tf_op jit(solution)/shard_map/dot_general | solution.py:25
  26.2 0.0 all-gather.3.cloned.1.call-update
  26.2 0.0 copy-done.5
  26.2 0.2 copy.26
  26.5 4.3 %stack.2 = bf16[16,1024,256]{1,2,0:T(8,128)(2,1)} broadcast(bf16[1024,256]{0,1:T(8,128)(2,1)S(1)} %copy.26), dimensions={1,2} | broadcast | bytes 8912896 | tf_op jit(solution)/shard_map/stack | solution.py:14
  30.8 0.0 copy-start.4
  30.8 8.3 %all-to-all-start = ((bf16[16,1024,256]{1,2,0:T(8,128)(2,1)}), bf16[16,1024,256]{1,2,0:T(8,128)(2,1)}, u32[]{:S(2)}, u32[]{:S(2)}) async-start(bf16[16,1024,256]{1,2,0:T(8,128)(2,1)} %stack.2), calls=%async_computation | async-start | bytes 16777216 | tf_op jit(solution)/shard_map/all_to_all | solution.py:15
  39.1 0.2 all-gather.5.cloned.1.call-start
  39.3 0.7 gather_fusion.1
  40.1 153.4 %all-to-all-done = bf16[16,1024,256]{1,2,0:T(8,128)(2,1)} async-done(((bf16[16,1024,256]{1,2,0:T(8,128)(2,1)}), bf16[16,1024,256]{1,2,0:T(8,128)(2,1)}, u32[]{:S(2)}, u32[]{:S(2)}) %all-to-all-start) | async-done | bytes 8388640 | tf_op jit(solution)/shard_map/all_to_all | solution.py:15
  193.5 0.0 copy-done.4
  193.5 5.8 %convolution_convert_fusion.3 = bf16[1024,256]{1,0:T(8,128)(2,1)S(1)} fusion(bf16[1024,4096]{0,1:T(8,128)(2,1)} %bitcast.8, bf16[4096,256]{1,0:T(8,128)(2,1)S(1)} %copy-done.4), kind=kOutput, calls=%fused_computation.62 | convolution fusion | flops 2147745792 | bytes 11010048 | tf_op jit(solution)/shard_map/dot_general | solution.py:60
  199.3 0.1 reshape.125
  199.4 13.0 %all-gather.3.cloned.1.call-done = bf16[4096,1024]{1,0:T(8,128)(2,1)} async-done(((bf16[256,1024]{1,0:T(8,128)(2,1)}), bf16[4096,1024]{1,0:T(8,128)(2,1)}) %all-gather.3.cloned.1.call-update) | async-done | bytes 8388624 | tf_op jit(solution)/shard_map/all_gather | solution.py:65
  212.4 10.1 %convolution_convert_fusion = bf16[4096,512]{1,0:T(8,128)(2,1)} fusion(bf16[4096,1024]{1,0:T(8,128)(2,1)} %all-gather.3.cloned.1.call-done, bf16[1024,256]{1,0:T(8,128)(2,1)} %param.12, bf16[1024,256]{1,0:T(8,128)(2,1)} %param.11), kind=kOutput, calls=%fused_computation.5 | convolution fusion | flops 4299161600 | bytes 13631488 | tf_op jit(solution)/shard_map/dot_general | solution.py:64
  222.5 4.9 %gather_fusion.2 = bf16[32,128,512]{2,1,0:T(8,128)(2,1)} fusion(bf16[32,128,512]{2,1,0:T(8,128)(2,1)} %bitcast.43, s32[1024]{0:T(1024)S(1)} %pad_clamp_fusion), kind=kCustom, calls=%fused_computation.2 | custom fusion | bytes 8388736 | tf_op jit(solution)/shard_map/gather | solution.py:71
  227.4 4.0 %fusion.104 = (bf16[16,256,256]{2,1,0:T(8,128)(2,1)}, bf16[16,256,256]{2,1,0:T(8,128)(2,1)S(1)}) fusion(bf16[16,256,512]{2,1,0:T(8,128)(2,1)} %bitcast.38), kind=kLoop, calls=%fused_computation.137 | loop fusion | bytes 8388608 | tf_op jit(solution)/shard_map/slice | solution.py:72
  231.4 2.4 copy.25
  233.8 2.8 copy.27
  236.6 0.4 fusion.56
  237.1 0.0 copy-start.3
  237.1 0.8 fusion.105
  237.8 0.5 copy-done.3
  238.4 0.0 copy-start.2
  238.4 6.0 %fusion.50 = bf16[16,64,2,128]{3,1,2,0:T(8,128)(2,1)S(1)} fusion(bf16[16,256,2,128]{1,3,2,0:T(8,128)(2,1)} %bitcast.44, f32[16,2,64]{2,1,0:T(2,128)S(1)} %fusion.105, f32[16,2,64,256]{3,2,1,0:T(8,128)} %copy-done.3), kind=kOutput, calls=%fused_computation.64 | convolution fusion | flops 136579328 | bytes 4726784 | tf_op jit(solution)/shard_map/chqk,ckhd->cqhd/dot_general | solution.py:81
  244.4 0.5 copy.31
  244.9 0.9 copy.40
  245.8 0.0 all-gather.5.cloned.1.call-update
  245.8 0.0 copy-done.2
  245.9 2.5 copy.32
  248.4 43.1 %all_to_all.24 = bf16[256,16,256]{0,2,1:T(8,128)(2,1)S(1)} all-to-all(bf16[256,16,256]{0,2,1:T(8,128)(2,1)} %bitcast.41), channel_id=1, replica_groups=mesh['sa'=8,'an'=16] {'an'}, dimensions={1} | all-to-all | bytes 4194304 | tf_op jit(solution)/shard_map/all_to_all | solution.py:85
  291.5 2.4 copy.33
  293.9 47.9 %all-gather.5.cloned.1.call-done = bf16[1024,4096]{1,0:T(8,128)(2,1)} async-done(((bf16[1024,256]{1,0:T(8,128)(2,1)}), bf16[1024,4096]{1,0:T(8,128)(2,1)}) %all-gather.5.cloned.1.call-update) | async-done | bytes 8388624 | tf_op jit(solution)/shard_map/all_gather | solution.py:88
  341.8 0.0 copy-start.1
  341.8 7.2 %convolution_convert_fusion.1 = bf16[1024,256]{1,0:T(8,128)(2,1)} fusion(bf16[1024,4096]{1,0:T(8,128)(2,1)} %all-gather.5.cloned.1.call-done, bf16[4096,256]{1,0:T(8,128)(2,1)} %bitcast.45), kind=kOutput, calls=%fused_computation.60 | convolution fusion | flops 2147745792 | bytes 11010048 | tf_op jit(solution)/shard_map/dot_general | solution.py:87
  349.0 0.0 copy-done.1
  (10 shorter events, 0.1 us)
Async XLA Ops:
  6.5 1.6 copy-start
  6.5 205.9 %all-gather.3.cloned.1.call-start = ((), (), s32[]{:S(2)}) async-start(), calls=%async_computation.2 | async-start | bytes 8912896 | tf_op jit(solution)/shard_map/all_gather | solution.py:65
  9.1 17.1 %copy-start.5 = (bf16[1024,256]{1,0:T(8,128)(2,1)S(1)}, bf16[1024,256]{1,0:T(8,128)(2,1)}, u32[]{:S(2)}) copy-start(bf16[1024,256]{1,0:T(8,128)(2,1)} %param.9) | copy-start | bytes 1572868
  30.8 162.7 %copy-start.4 = (bf16[4096,256]{1,0:T(8,128)(2,1)S(1)}, bf16[4096,256]{1,0:T(8,128)(2,1)}, u32[]{:S(2)}) copy-start(bf16[4096,256]{1,0:T(8,128)(2,1)} %param.10) | copy-start | bytes 6291460
  30.8 162.7 %all-to-all-start = ((bf16[16,1024,256]{1,2,0:T(8,128)(2,1)}), bf16[16,1024,256]{1,2,0:T(8,128)(2,1)}, u32[]{:S(2)}, u32[]{:S(2)}) async-start(bf16[16,1024,256]{1,2,0:T(8,128)(2,1)} %stack.2), calls=%async_computation | async-start | bytes 16777216 | tf_op jit(solution)/shard_map/all_to_all | solution.py:15
  39.1 302.7 %all-gather.5.cloned.1.call-start = ((), (), s32[]{:S(2)}) async-start(), calls=%async_computation.3 | async-start | bytes 8912896 | tf_op jit(solution)/shard_map/all_gather | solution.py:88
  237.1 1.3 copy-start.3
  238.4 7.5 %copy-start.2 = (bf16[256,4096]{1,0:T(8,128)(2,1)S(1)}, bf16[256,4096]{1,0:T(8,128)(2,1)}, u32[]{:S(2)}) copy-start(bf16[256,4096]{1,0:T(8,128)(2,1)} %param.13) | copy-start | bytes 6291460
  341.8 7.3 %copy-start.1 = (bf16[8,128,1024]{2,1,0:T(8,128)(2,1)S(1)}, bf16[8,128,1024]{2,1,0:T(8,128)(2,1)}, u32[]{:S(2)}) copy-start(bf16[8,128,1024]{2,1,0:T(8,128)(2,1)} %param.16) | copy-start | bytes 6291460
Sparse Core Ops, SparseCore 0:
  26.4 186.0 all-gather.2
  246.0 95.7 all-gather.4
